TPU v7x, 32 devices: a whole 2x2x4 slice. The times are simulated.
32 devices in a mesh: scen: 8 (over y, x, core), col: 4 (over z).
Axes of the slice: x: 2, y: 2, z: 4, core: 2. Of those that a mesh axis runs over, the one named last changes fastest.
Arguments:
- tech: bfloat16 [32, 2048, 4096], P('scen', None, 'col'), may hold values from -0.046875 to 0.046875
- recourse: bfloat16 [32, 2048, 1024], P('scen', None, 'col'), may hold values from -0.125 to 0.125
- rhs: float32 [32, 32, 2048], P(None, 'scen'), may hold values from -6 to 6
- cost_first: float32 [4096], P('col'), may hold values from -6 to 6
- cost_second: float32 [32, 1024], P('scen', 'col'), may hold values from -6 to 6
- cone_id: int32 [32, 2048], P('scen'), may hold values from 0 to 127, never falling along the last dimension, each value on 1 to 64 neighbouring positions
Outputs:
- first_section: float32 [32, 4096], P(None, 'col')
- second_section: float32 [32, 32, 1024], P(None, 'scen', 'col')
- slack: float32 [32, 32, 2048], P(None, 'scen', 'col')
- dual: float32 [32, 32, 2048], P(None, 'scen', 'col')
Inputs may be any that keep to these rules, and one draw needn't show every extreme that they name: Along the rows of a scenario cone_id never falls; a cone holds 1 to 64 rows.
All inputs are finite; a program needn't handle non-finite values.
Results may differ from a plain program's by a relative error of at most 0.014.
Values may be sent and summed in bfloat16 or wider, within the bound.
A program may use at most 128 MiB of HBM per device.

v0:
```python
import jax
import jax.numpy as jnp
from jax import lax
from jax.sharding import PartitionSpec as P

NCONE = 128
ITERS = 3
CG_STEPS = 3
HIGH = lax.Precision.HIGHEST


def cone_factors(lead, tail):
    norm_tail = jnp.sqrt(tail)
    inside = norm_tail <= lead
    polar = norm_tail <= -lead
    safe = jnp.where(norm_tail > 0.0, norm_tail, 1.0)
    middle = 0.5 * (lead + norm_tail)
    head = jnp.where(inside, lead, jnp.where(polar, 0.0, middle))
    scale = jnp.where(inside, 1.0, jnp.where(polar, 0.0, middle / safe))
    return (head, scale)


def body(tech, recourse, rhs, cost_first, cost_second, cone_id):
    f32 = jnp.float32
    bf16 = jnp.bfloat16
    n_scen = lax.axis_size("scen")
    n_col = lax.axis_size("col")
    batch = rhs.shape[0]
    scen_local = tech.shape[0]
    rows = tech.shape[1]
    first_cols = tech.shape[2]
    tech_flat = tech.reshape(scen_local * rows, first_cols)
    starts = jnp.concatenate(
        [jnp.ones((scen_local, 1), f32), (cone_id[:, 1:] != cone_id[:, :-1]).astype(f32)], axis=1
    )
    labels = lax.broadcasted_iota(jnp.int32, (1, 1, NCONE), 2)
    onehot = (cone_id[:, :, None] == labels).astype(f32)
    part_rows = rows // n_col
    row_start = lax.axis_index("col") * part_rows
    row_weight = 1.0 / n_col
    share_cols = first_cols // n_scen
    cost_here = lax.dynamic_slice_in_dim(
        cost_first, lax.axis_index("scen") * share_cols, share_cols, 0
    )
    first_weight = 1.0
    start_rows = starts[None]

    def couple(partial_value):
        return lax.psum_scatter(partial_value, "scen", scatter_dimension=1, tiled=True)

    def adjoint(rows_bf):
        first_part = jnp.dot(
            rows_bf.reshape(batch, scen_local * rows), tech_flat, preferred_element_type=f32
        )
        second_part = jnp.einsum("bsm,smk->bsk", rows_bf, recourse, preferred_element_type=f32)
        return (first_part, second_part)

    def local_squares(first_vec, second_vec):
        return first_weight * jnp.sum(first_vec * first_vec, axis=1) + jnp.sum(
            second_vec * second_vec, axis=(1, 2)
        )

    def total_norm(first_vec, second_vec):
        return lax.psum(local_squares(first_vec, second_vec), ("scen", "col"))

    here_rows = rhs.shape[2]
    first_sol = jnp.zeros((batch, share_cols), f32)
    second_sol = jnp.zeros((batch, scen_local, recourse.shape[2]), f32)
    slack = jnp.zeros((batch, scen_local, here_rows), f32)
    dual = jnp.zeros((batch, scen_local, here_rows), f32)
    image = jnp.zeros((batch, scen_local, here_rows), f32)
    for outer in range(ITERS):
        resid_rows = (rhs - slack - dual - image).astype(bf16)
        back_first, back_second = adjoint(resid_rows)
        res_first = couple(back_first) - cost_here[None, :]
        res_second = back_second - cost_second[None]
        res_norm = total_norm(res_first, res_second)
        dir_first, dir_second = (res_first, res_second)
        for step in range(CG_STEPS):
            dir_first_bf = lax.all_gather(dir_first.astype(bf16), "scen", axis=1, tiled=True)
            forward_partial_value = lax.dot_general(
                dir_first_bf, tech_flat, (((1,), (1,)), ((), ())), preferred_element_type=f32
            )
            forward_partial_value = forward_partial_value.reshape(batch, scen_local, rows)
            image_step = lax.psum(
                forward_partial_value
                + jnp.einsum(
                    "bsk,smk->bsm", dir_second.astype(bf16), recourse, preferred_element_type=f32
                ),
                "col",
            )
            curv_term = local_squares(dir_first, dir_second) + row_weight * jnp.sum(
                image_step * image_step, axis=(1, 2)
            )
            curv = lax.psum(curv_term, ("scen", "col"))
            alpha = res_norm / curv
            first_sol = first_sol + alpha[:, None] * dir_first
            second_sol = second_sol + alpha[:, None, None] * dir_second
            image = image + alpha[:, None, None] * image_step
            if step + 1 < CG_STEPS:
                back_first, back_second = adjoint(image_step.astype(bf16))
                res_first = res_first - alpha[:, None] * (dir_first + couple(back_first))
                res_second = res_second - alpha[:, None, None] * (dir_second + back_second)
                new_norm = total_norm(res_first, res_second)
                ratio = new_norm / res_norm
                dir_first = res_first + ratio[:, None] * dir_first
                dir_second = res_second + ratio[:, None, None] * dir_second
                res_norm = new_norm
        values = rhs - image - dual
        project_lead = jnp.einsum("bsm,smc->bsc", values * start_rows, onehot, precision=HIGH)
        project_tail = jnp.einsum(
            "bsm,smc->bsc", values * values * (1.0 - start_rows), onehot, precision=HIGH
        )
        project_lead, project_tail = (project_lead, project_tail)
        head, scale = cone_factors(project_lead, project_tail)
        head_rows = jnp.einsum("bsc,smc->bsm", head, onehot, precision=HIGH)
        scale_rows = jnp.einsum("bsc,smc->bsm", scale, onehot, precision=HIGH)
        slack = start_rows * head_rows + (1.0 - start_rows) * values * scale_rows
        dual = dual + image + slack - rhs
    first_out = lax.all_gather(first_sol, "scen", axis=1, tiled=True)
    slack_out = lax.dynamic_slice_in_dim(slack, row_start, part_rows, 2)
    dual_out = lax.dynamic_slice_in_dim(dual, row_start, part_rows, 2)
    return (first_out, second_sol, slack_out, dual_out)


def solution(mesh):
    placed = (
        P("scen", None, "col"),
        P("scen", None, "col"),
        P(None, "scen", None),
        P("col"),
        P("scen", "col"),
        P("scen", None),
    )
    return jax.shard_map(
        body,
        mesh=mesh,
        in_specs=placed,
        out_specs=(
            P(None, "col"),
            P(None, "scen", "col"),
            P(None, "scen", "col"),
            P(None, "scen", "col"),
        ),
        check_vma=False,
    )
```

profile of v0, /device:TPU:0, one launch (start us, length us, event | category | flops | bytes accessed | tf_op | source)
XLA Modules:
  0.0 1593.4 jit_solution(15257409397023678679)
XLA Ops:
  22.1 32.4 %reduce-scatter.10.cloned.1.call-done = f32[32,128]{1,0:T(8,128)} async-done(((f32[32,1024]{1,0:T(8,128)}), f32[32,128]{1,0:T(8,128)}) %reduce-scatter.10.cloned.1.call-update) | async-done | bytes 16400 | tf_op jit(solution)/shard_map/reduce_scatter | solution.py:49
  64.2 12.0 fusion.136
  79.9 52.0 %all-reduce.14.cloned.1.call-done = f32[32,4,2048]{2,0,1:T(8,128)} async-done(((f32[32,4,2048]{2,0,1:T(8,128)}), f32[32,4,2048]{2,0,1:T(8,128)}) %all-reduce.14.cloned.1.call-update) | async-done | bytes 1048592 | tf_op jit(solution)/shard_map/psum | solution.py:85
  131.9 9.8 convolution_bitcast_fusion.22
  142.0 40.0 %all-reduce.3 = (f32[32]{0:T(128)S(1)}, f32[32]{0:T(128)S(1)}) all-reduce(f32[32]{0:T(128)S(1)} %get-tuple-element.49, f32[32]{0:T(128)S(1)} %get-tuple-element.48), channel_id=1, replica_groups=mesh['scen'=8,'col'=4] {'scen','col'}, use_global_device_ids=true, to_apply=%region_3.0 | all-reduce | flops 64 | bytes 512 | tf_op jit(solution)/shard_map/psum | solution.py:64
  186.0 39.4 %psum.192 = f32[32]{0:T(128)S(1)} all-reduce(f32[32]{0:T(128)S(1)} %add.364), channel_id=1, replica_groups=mesh['scen'=8,'col'=4] {'scen','col'}, use_global_device_ids=true, to_apply=%region_10.0 | all-reduce | flops 32 | bytes 256 | tf_op jit(solution)/shard_map/psum | solution.py:64
  235.3 11.9 fusion.134
  251.0 50.4 %all-reduce.16.cloned.1.call-done = f32[32,4,2048]{2,0,1:T(8,128)} async-done(((f32[32,4,2048]{2,0,1:T(8,128)}), f32[32,4,2048]{2,0,1:T(8,128)}) %all-reduce.16.cloned.1.call-update) | async-done | bytes 1048592 | tf_op jit(solution)/shard_map/psum | solution.py:85
  302.9 9.8 convolution_bitcast_fusion.21
  312.7 40.0 %psum.194 = f32[32]{0:T(128)S(1)} all-reduce(f32[32]{0:T(128)S(1)} %multiply_add_fusion.27), channel_id=1, replica_groups=mesh['scen'=8,'col'=4] {'scen','col'}, use_global_device_ids=true, to_apply=%region_15.0 | all-reduce | flops 32 | bytes 256 | tf_op jit(solution)/shard_map/psum | solution.py:95
  356.8 39.2 %psum.195 = f32[32]{0:T(128)S(1)} all-reduce(f32[32]{0:T(128)S(1)} %add.373), channel_id=1, replica_groups=mesh['scen'=8,'col'=4] {'scen','col'}, use_global_device_ids=true, to_apply=%region_19.0 | all-reduce | flops 32 | bytes 256 | tf_op jit(solution)/shard_map/psum | solution.py:64
  396.9 10.1 all_gather.32
  407.0 11.9 fusion.132
  422.9 50.0 %all-reduce.18.cloned.1.call-done = f32[32,4,2048]{2,0,1:T(8,128)} async-done(((f32[32,4,2048]{2,0,1:T(8,128)}), f32[32,4,2048]{2,0,1:T(8,128)}) %all-reduce.18.cloned.1.call-update) | async-done | bytes 1048592 | tf_op jit(solution)/shard_map/psum | solution.py:85
  474.5 40.0 %psum.197 = f32[32]{0:T(128)S(1)} all-reduce(f32[32]{0:T(128)S(1)} %multiply_add_fusion.26), channel_id=1, replica_groups=mesh['scen'=8,'col'=4] {'scen','col'}, use_global_device_ids=true, to_apply=%region_24.0 | all-reduce | flops 32 | bytes 256 | tf_op jit(solution)/shard_map/psum | solution.py:95
  542.3 29.9 %reduce-scatter.16.cloned.1.call-done = f32[32,128]{1,0:T(8,128)} async-done(((f32[32,1024]{1,0:T(8,128)}), f32[32,128]{1,0:T(8,128)}) %reduce-scatter.16.cloned.1.call-update) | async-done | bytes 16400 | tf_op jit(solution)/shard_map/reduce_scatter | solution.py:49
  582.0 11.9 fusion.130
  597.5 52.0 %all-reduce.20.cloned.1.call-done = f32[32,4,2048]{2,0,1:T(8,128)} async-done(((f32[32,4,2048]{2,0,1:T(8,128)}), f32[32,4,2048]{2,0,1:T(8,128)}) %all-reduce.20.cloned.1.call-update) | async-done | bytes 1048592 | tf_op jit(solution)/shard_map/psum | solution.py:85
  649.5 9.8 convolution_bitcast_fusion.19
  659.7 40.0 %all-reduce.2 = (f32[32]{0:T(128)S(1)}, f32[32]{0:T(128)S(1)}) all-reduce(f32[32]{0:T(128)S(1)} %get-tuple-element.39, f32[32]{0:T(128)S(1)} %get-tuple-element.38), channel_id=1, replica_groups=mesh['scen'=8,'col'=4] {'scen','col'}, use_global_device_ids=true, to_apply=%region_28.29 | all-reduce | flops 64 | bytes 512 | tf_op jit(solution)/shard_map/psum | solution.py:64
  703.7 39.2 %psum.201 = f32[32]{0:T(128)S(1)} all-reduce(f32[32]{0:T(128)S(1)} %add.391), channel_id=1, replica_groups=mesh['scen'=8,'col'=4] {'scen','col'}, use_global_device_ids=true, to_apply=%region_35.36 | all-reduce | flops 32 | bytes 256 | tf_op jit(solution)/shard_map/psum | solution.py:64
  743.0 9.9 all_gather.34
  752.9 11.9 fusion.128
  768.7 50.4 %all-reduce.22.cloned.1.call-done = f32[32,4,2048]{2,0,1:T(8,128)} async-done(((f32[32,4,2048]{2,0,1:T(8,128)}), f32[32,4,2048]{2,0,1:T(8,128)}) %all-reduce.22.cloned.1.call-update) | async-done | bytes 1048592 | tf_op jit(solution)/shard_map/psum | solution.py:85
  820.5 9.8 convolution_bitcast_fusion.18
  830.4 40.0 %psum.203 = f32[32]{0:T(128)S(1)} all-reduce(f32[32]{0:T(128)S(1)} %multiply_add_fusion.24), channel_id=1, replica_groups=mesh['scen'=8,'col'=4] {'scen','col'}, use_global_device_ids=true, to_apply=%region_40.41 | all-reduce | flops 32 | bytes 256 | tf_op jit(solution)/shard_map/psum | solution.py:95
  874.5 39.2 %psum.204 = f32[32]{0:T(128)S(1)} all-reduce(f32[32]{0:T(128)S(1)} %add.400), channel_id=1, replica_groups=mesh['scen'=8,'col'=4] {'scen','col'}, use_global_device_ids=true, to_apply=%region_44.45 | all-reduce | flops 32 | bytes 256 | tf_op jit(solution)/shard_map/psum | solution.py:64
  915.2 10.1 all_gather.35
  925.2 11.9 fusion.126
  941.0 50.3 %all-reduce.24.cloned.1.call-done = f32[32,4,2048]{2,0,1:T(8,128)} async-done(((f32[32,4,2048]{2,0,1:T(8,128)}), f32[32,4,2048]{2,0,1:T(8,128)}) %all-reduce.24.cloned.1.call-update) | async-done | bytes 1048592 | tf_op jit(solution)/shard_map/psum | solution.py:85
  992.7 40.0 %psum.206 = f32[32]{0:T(128)S(1)} all-reduce(f32[32]{0:T(128)S(1)} %multiply_add_fusion.23), channel_id=1, replica_groups=mesh['scen'=8,'col'=4] {'scen','col'}, use_global_device_ids=true, to_apply=%region_49.50 | all-reduce | flops 32 | bytes 256 | tf_op jit(solution)/shard_map/psum | solution.py:95
  1061.9 29.9 %reduce-scatter.22.cloned.1.call-done = f32[32,128]{1,0:T(8,128)} async-done(((f32[32,1024]{1,0:T(8,128)}), f32[32,128]{1,0:T(8,128)}) %reduce-scatter.22.cloned.1.call-update) | async-done | bytes 16400 | tf_op jit(solution)/shard_map/reduce_scatter | solution.py:49
  1101.6 11.9 fusion.124
  1117.1 52.0 %all-reduce.26.cloned.1.call-done = f32[32,4,2048]{2,0,1:T(8,128)} async-done(((f32[32,4,2048]{2,0,1:T(8,128)}), f32[32,4,2048]{2,0,1:T(8,128)}) %all-reduce.26.cloned.1.call-update) | async-done | bytes 1048592 | tf_op jit(solution)/shard_map/psum | solution.py:85
  1169.1 9.8 convolution_bitcast_fusion.16
  1179.3 40.0 %all-reduce.1 = (f32[32]{0:T(128)S(1)}, f32[32]{0:T(128)S(1)}) all-reduce(f32[32]{0:T(128)S(1)} %get-tuple-element.25, f32[32]{0:T(128)S(1)} %get-tuple-element.24), channel_id=1, replica_groups=mesh['scen'=8,'col'=4] {'scen','col'}, use_global_device_ids=true, to_apply=%region_53.54 | all-reduce | flops 64 | bytes 512 | tf_op jit(solution)/shard_map/psum | solution.py:64
  1223.3 39.2 %psum.210 = f32[32]{0:T(128)S(1)} all-reduce(f32[32]{0:T(128)S(1)} %add.420), channel_id=1, replica_groups=mesh['scen'=8,'col'=4] {'scen','col'}, use_global_device_ids=true, to_apply=%region_60.61 | all-reduce | flops 32 | bytes 256 | tf_op jit(solution)/shard_map/psum | solution.py:64
  1262.7 9.9 all_gather.37
  1272.5 11.9 fusion.122
  1288.4 50.4 %all-reduce.28.cloned.1.call-done = f32[32,4,2048]{2,0,1:T(8,128)} async-done(((f32[32,4,2048]{2,0,1:T(8,128)}), f32[32,4,2048]{2,0,1:T(8,128)}) %all-reduce.28.cloned.1.call-update) | async-done | bytes 1048592 | tf_op jit(solution)/shard_map/psum | solution.py:85
  1340.2 9.8 convolution_bitcast_fusion.15
  1350.1 40.0 %psum.212 = f32[32]{0:T(128)S(1)} all-reduce(f32[32]{0:T(128)S(1)} %multiply_add_fusion.21), channel_id=1, replica_groups=mesh['scen'=8,'col'=4] {'scen','col'}, use_global_device_ids=true, to_apply=%region_65.66 | all-reduce | flops 32 | bytes 256 | tf_op jit(solution)/shard_map/psum | solution.py:95
  1394.2 39.2 %psum.213 = f32[32]{0:T(128)S(1)} all-reduce(f32[32]{0:T(128)S(1)} %add.429), channel_id=1, replica_groups=mesh['scen'=8,'col'=4] {'scen','col'}, use_global_device_ids=true, to_apply=%region_69.70 | all-reduce | flops 32 | bytes 256 | tf_op jit(solution)/shard_map/psum | solution.py:64
  1435.4 9.9 all_gather.38
  1445.3 11.9 fusion.120
  1462.7 48.7 %all-reduce.30.cloned.1.call-done = f32[32,4,2048]{2,0,1:T(8,128)} async-done(((f32[32,4,2048]{2,0,1:T(8,128)}), f32[32,4,2048]{2,0,1:T(8,128)}) %all-reduce.30.cloned.1.call-update) | async-done | bytes 1048592 | tf_op jit(solution)/shard_map/psum | solution.py:85
  1514.0 40.1 %psum.215 = f32[32]{0:T(128)} all-reduce(f32[32]{0:T(128)} %multiply_add_fusion.20), channel_id=1, replica_groups=mesh['scen'=8,'col'=4] {'scen','col'}, use_global_device_ids=true, to_apply=%region_74.75 | all-reduce | flops 32 | bytes 256 | tf_op jit(solution)/shard_map/psum | solution.py:95
  1557.0 10.3 all_gather.39
  (276 shorter events, 208.2 us)
Async XLA Ops:
  7.2 47.4 %reduce-scatter.10.cloned.1.call-start = ((), (), s32[]{:S(2)}) async-start(), calls=%async_computation.9 | async-start | bytes 147456 | tf_op jit(solution)/shard_map/reduce_scatter | solution.py:49
  18.1 113.7 %all-reduce.14.cloned.1.call-start = ((), (), s32[]{:S(2)}) async-start(), calls=%async_computation.10 | async-start | bytes 2097152 | tf_op jit(solution)/shard_map/psum | solution.py:85
  18.9 1243.5 %copy-start.43 = (f32[128]{0:T(128)}, f32[128]{0:T(128)S(1)}, u32[]{:S(2)}) copy-start(f32[128]{0:T(128)S(1)} %dynamic_slice.9) | copy-start | bytes 1540
  22.1 225.1 %copy-start.24 = (f32[32,4,256]{2,0,1:T(8,128)}, f32[32,4,256]{2,0,1:T(8,128)S(1)}, u32[]{:S(2)}) copy-start(f32[32,4,256]{2,0,1:T(8,128)S(1)} %get-tuple-element.60) | copy-start | bytes 393220
  79.8 105.3 %reduce-scatter.12.cloned.1.call-start = ((), (), s32[]{:S(2)}) async-start(), calls=%async_computation.11 | async-start | bytes 147456 | tf_op jit(solution)/shard_map/reduce_scatter | solution.py:49
  141.7 43.4 %copy-start.37 = (f32[32,128]{1,0:T(8,128)S(1)}, f32[32,128]{1,0:T(8,128)}, u32[]{:S(2)}) copy-start(f32[32,128]{1,0:T(8,128)} %reduce-scatter.10.cloned.1.call-done) | copy-start | bytes 49156
  141.7 159.7 %all-reduce.16.cloned.1.call-start = ((), (), s32[]{:S(2)}) async-start(), calls=%async_computation.12 | async-start | bytes 2097152 | tf_op jit(solution)/shard_map/psum | solution.py:85
  181.9 332.5 %copy-start.49 = (f32[32]{0:T(128)}, f32[32]{0:T(128)S(1)}, u32[]{:S(2)}) copy-start(f32[32]{0:T(128)S(1)} %div.54) | copy-start | bytes 388
  251.0 104.9 %reduce-scatter.14.cloned.1.call-start = ((), (), s32[]{:S(2)}) async-start(), calls=%async_computation.13 | async-start | bytes 147456 | tf_op jit(solution)/shard_map/reduce_scatter | solution.py:49
  302.8 49.9 %copy-start.20 = (f32[32,4,2048]{2,0,1:T(8,128)S(1)}, f32[32,4,2048]{2,0,1:T(8,128)}, u32[]{:S(2)}) copy-start(f32[32,4,2048]{2,0,1:T(8,128)} %all-reduce.16.cloned.1.call-done) | copy-start | bytes 3145732
  312.7 160.3 %all-reduce.18.cloned.1.call-start = ((), (), s32[]{:S(2)}) async-start(), calls=%async_computation.14 | async-start | bytes 2097152 | tf_op jit(solution)/shard_map/psum | solution.py:85
  352.7 161.8 %copy-start.46 = (f32[32]{0:T(128)}, f32[32]{0:T(128)S(1)}, u32[]{:S(2)}) copy-start(f32[32]{0:T(128)S(1)} %div.56) | copy-start | bytes 388
  355.8 66.9 %copy-start.27 = (f32[32,4,256]{2,0,1:T(8,128)}, f32[32,4,256]{2,0,1:T(8,128)S(1)}, u32[]{:S(2)}) copy-start(f32[32,4,256]{2,0,1:T(8,128)S(1)} %get-tuple-element.64) | copy-start | bytes 393220
  396.0 26.8 %copy-start.52 = (f32[32]{0:T(128)}, f32[32]{0:T(128)S(1)}, u32[]{:S(2)}) copy-start(f32[32]{0:T(128)S(1)} %div.57) | copy-start | bytes 388
  422.4 94.2 %copy-start.9 = (f32[32,4,2048]{2,1,0:T(4,128)S(1)}, f32[32,4,2048]{2,1,0:T(4,128)}, u32[]{:S(2)}) copy-start(f32[32,4,2048]{2,1,0:T(4,128)} %param.8) | copy-start | bytes 3145732
  422.5 149.7 %reduce-scatter.16.cloned.1.call-start = ((), (), s32[]{:S(2)}) async-start(), calls=%async_computation.15 | async-start | bytes 147456 | tf_op jit(solution)/shard_map/reduce_scatter | solution.py:49
  422.7 618.7 %copy-start.44 = (f32[4,2048]{1,0:T(4,128)}, f32[4,2048]{1,0:T(4,128)S(1)}, u32[]{:S(2)}) copy-start(f32[4,2048]{1,0:T(4,128)S(1)} %broadcast_subtract_fusion) | copy-start | bytes 98308
  474.5 570.3 %copy-start.35 = (f32[4,2048]{1,0:T(4,128)}, f32[4,2048]{1,0:T(4,128)S(1)}, u32[]{:S(2)}) copy-start(f32[4,2048]{1,0:T(4,128)S(1)} %pad_convert_fusion) | copy-start | bytes 98308
  539.1 110.4 %all-reduce.20.cloned.1.call-start = ((), (), s32[]{:S(2)}) async-start(), calls=%async_computation.16 | async-start | bytes 2097152 | tf_op jit(solution)/shard_map/psum | solution.py:85
  542.3 222.6 %copy-start.25 = (f32[32,4,256]{2,0,1:T(8,128)}, f32[32,4,256]{2,0,1:T(8,128)S(1)}, u32[]{:S(2)}) copy-start(f32[32,4,256]{2,0,1:T(8,128)S(1)} %get-tuple-element.70) | copy-start | bytes 393220
  597.5 105.3 %reduce-scatter.18.cloned.1.call-start = ((), (), s32[]{:S(2)}) async-start(), calls=%async_computation.17 | async-start | bytes 147456 | tf_op jit(solution)/shard_map/reduce_scatter | solution.py:49
  659.4 43.4 %copy-start.38 = (f32[32,128]{1,0:T(8,128)S(1)}, f32[32,128]{1,0:T(8,128)}, u32[]{:S(2)}) copy-start(f32[32,128]{1,0:T(8,128)} %reduce-scatter.16.cloned.1.call-done) | copy-start | bytes 49156
  659.4 159.7 %all-reduce.22.cloned.1.call-start = ((), (), s32[]{:S(2)}) async-start(), calls=%async_computation.18 | async-start | bytes 2097152 | tf_op jit(solution)/shard_map/psum | solution.py:85
  699.6 333.1 %copy-start.50 = (f32[32]{0:T(128)}, f32[32]{0:T(128)S(1)}, u32[]{:S(2)}) copy-start(f32[32]{0:T(128)S(1)} %div.60) | copy-start | bytes 388
  743.0 170.6 %copy-start.33 = (f32[32,128]{1,0:T(8,128)}, f32[32,128]{1,0:T(8,128)S(1)}, u32[]{:S(2)}) copy-start(f32[32,128]{1,0:T(8,128)S(1)} %get-tuple-element.35) | copy-start | bytes 49156
  768.6 104.9 %reduce-scatter.20.cloned.1.call-start = ((), (), s32[]{:S(2)}) async-start(), calls=%async_computation.19 | async-start | bytes 147456 | tf_op jit(solution)/shard_map/reduce_scatter | solution.py:49
  820.5 49.9 %copy-start.21 = (f32[32,4,2048]{2,0,1:T(8,128)S(1)}, f32[32,4,2048]{2,0,1:T(8,128)}, u32[]{:S(2)}) copy-start(f32[32,4,2048]{2,0,1:T(8,128)} %all-reduce.22.cloned.1.call-done) | copy-start | bytes 3145732
  830.4 160.9 %all-reduce.24.cloned.1.call-start = ((), (), s32[]{:S(2)}) async-start(), calls=%async_computation.20 | async-start | bytes 2097152 | tf_op jit(solution)/shard_map/psum | solution.py:85
  870.4 162.3 %copy-start.47 = (f32[32]{0:T(128)}, f32[32]{0:T(128)S(1)}, u32[]{:S(2)}) copy-start(f32[32]{0:T(128)S(1)} %div.62) | copy-start | bytes 388
  873.5 67.3 %copy-start.28 = (f32[32,4,256]{2,0,1:T(8,128)}, f32[32,4,256]{2,0,1:T(8,128)S(1)}, u32[]{:S(2)}) copy-start(f32[32,4,256]{2,0,1:T(8,128)S(1)} %get-tuple-element.74) | copy-start | bytes 393220
  913.6 27.2 %copy-start.53 = (f32[32]{0:T(128)}, f32[32]{0:T(128)S(1)}, u32[]{:S(2)}) copy-start(f32[32]{0:T(128)S(1)} %div.63) | copy-start | bytes 388
  940.8 151.0 %reduce-scatter.22.cloned.1.call-start = ((), (), s32[]{:S(2)}) async-start(), calls=%async_computation.21 | async-start | bytes 147456 | tf_op jit(solution)/shard_map/reduce_scatter | solution.py:49
  1058.7 110.4 %all-reduce.26.cloned.1.call-start = ((), (), s32[]{:S(2)}) async-start(), calls=%async_computation.22 | async-start | bytes 2097152 | tf_op jit(solution)/shard_map/psum | solution.py:85
  1061.9 222.6 %copy-start.26 = (f32[32,4,256]{2,0,1:T(8,128)}, f32[32,4,256]{2,0,1:T(8,128)S(1)}, u32[]{:S(2)}) copy-start(f32[32,4,256]{2,0,1:T(8,128)S(1)} %get-tuple-element.78) | copy-start | bytes 393220
  1117.1 105.3 %reduce-scatter.24.cloned.1.call-start = ((), (), s32[]{:S(2)}) async-start(), calls=%async_computation.23 | async-start | bytes 147456 | tf_op jit(solution)/shard_map/reduce_scatter | solution.py:49
  1179.0 43.4 %copy-start.39 = (f32[32,128]{1,0:T(8,128)S(1)}, f32[32,128]{1,0:T(8,128)}, u32[]{:S(2)}) copy-start(f32[32,128]{1,0:T(8,128)} %reduce-scatter.22.cloned.1.call-done) | copy-start | bytes 49156
  1179.0 159.8 %all-reduce.28.cloned.1.call-start = ((), (), s32[]{:S(2)}) async-start(), calls=%async_computation.24 | async-start | bytes 2097152 | tf_op jit(solution)/shard_map/psum | solution.py:85
  1219.2 43.2 %copy-start.51 = (f32[32]{0:T(128)}, f32[32]{0:T(128)S(1)}, u32[]{:S(2)}) copy-start(f32[32]{0:T(128)S(1)} %div.66) | copy-start | bytes 388
  1262.6 170.7 %copy-start.34 = (f32[32,128]{1,0:T(8,128)}, f32[32,128]{1,0:T(8,128)S(1)}, u32[]{:S(2)}) copy-start(f32[32,128]{1,0:T(8,128)S(1)} %get-tuple-element.21) | copy-start | bytes 49156
  1288.3 104.9 %reduce-scatter.26.cloned.1.call-start = ((), (), s32[]{:S(2)}) async-start(), calls=%async_computation.25 | async-start | bytes 147456 | tf_op jit(solution)/shard_map/reduce_scatter | solution.py:49
  1340.2 49.9 %copy-start.18 = (f32[32,4,2048]{2,0,1:T(8,128)S(1)}, f32[32,4,2048]{2,0,1:T(8,128)}, u32[]{:S(2)}) copy-start(f32[32,4,2048]{2,0,1:T(8,128)} %all-reduce.28.cloned.1.call-done) | copy-start | bytes 3145732
  1350.1 161.3 %all-reduce.30.cloned.1.call-start = ((), (), s32[]{:S(2)}) async-start(), calls=%async_computation.26 | async-start | bytes 2097152 | tf_op jit(solution)/shard_map/psum | solution.py:85
  1390.1 67.2 %copy-start.48 = (f32[32]{0:T(128)}, f32[32]{0:T(128)S(1)}, u32[]{:S(2)}) copy-start(f32[32]{0:T(128)S(1)} %div.68) | copy-start | bytes 388
  1393.2 64.1 %copy-start.29 = (f32[32,4,256]{2,0,1:T(8,128)}, f32[32,4,256]{2,0,1:T(8,128)S(1)}, u32[]{:S(2)}) copy-start(f32[32,4,256]{2,0,1:T(8,128)S(1)} %get-tuple-element.82) | copy-start | bytes 393220
  1433.3 24.0 %copy-start.57 = (f32[32]{0:T(128)}, f32[32]{0:T(128)S(1)}, u32[]{:S(2)}) copy-start(f32[32]{0:T(128)S(1)} %psum.213) | copy-start | bytes 388
  1460.9 107.2 %copy-start.11 = (f32[32,4,2048]{2,1,0:T(4,128)S(1)}, f32[32,4,2048]{2,1,0:T(4,128)}, u32[]{:S(2)}) copy-start(f32[32,4,2048]{2,1,0:T(4,128)} %param.8) | copy-start | bytes 3145732
  1460.9 107.2 %copy-start.15 = (f32[32,4,2048]{2,0,1:T(8,128)S(1)}, f32[32,4,2048]{2,0,1:T(8,128)}, u32[]{:S(2)}) copy-start(f32[32,4,2048]{2,0,1:T(8,128)} %all-reduce.26.cloned.1.call-done) | copy-start | bytes 3145732
  1460.9 107.2 %copy-start.19 = (f32[32,4,2048]{2,0,1:T(8,128)S(1)}, f32[32,4,2048]{2,0,1:T(8,128)}, u32[]{:S(2)}) copy-start(f32[32,4,2048]{2,0,1:T(8,128)} %all-reduce.28.cloned.1.call-done) | copy-start | bytes 3145732
  (28 other events, 255.4 us)
Sparse Core Ops, SparseCore 0:
  18.2 36.2 reduce-scatter.9
  79.9 51.8 all-reduce.13
  141.8 32.8 reduce-scatter.11
  251.1 50.3 all-reduce.15
  312.8 32.8 reduce-scatter.13
  422.6 50.3 all-reduce.17
  539.2 32.8 reduce-scatter.15
  597.6 51.8 all-reduce.19
  659.5 32.8 reduce-scatter.17
  768.7 50.3 all-reduce.21
  830.5 32.8 reduce-scatter.19
  940.9 50.3 all-reduce.23
  1058.9 32.8 reduce-scatter.21
  1117.2 51.8 all-reduce.25
  1179.1 32.8 reduce-scatter.23
  1288.4 50.3 all-reduce.27
  1350.2 32.8 reduce-scatter.25
  1461.0 50.3 all-reduce.29
where the time goes:
time: 1610 us; the launch traced here: 1590 us
  blocking collectives  692 us (43%)
  waiting for transfers between devices  549 us (34%)
  matrix products  292 us (18%)
  other arithmetic  39.5 us (2%)
    psum x9, waiting for transfers between devices, body(): lax.psum(forward_partial_value + jnp.einsum('bsk,smk->bsm', dir_second.as...  456 us
    psum x9, blocking collectives, total_norm(): return lax.psum(local_squares(first_vec, second_vec), ('scen', 'col'))  355 us
    psum x6, blocking collectives, body(): curv = lax.psum(curv_term, ('scen', 'col'))  240 us
    dot_general x9, matrix products, body(): lax.dot_general(dir_first_bf, tech_flat, (((1,), (1,)), ((), ())), prefer...  107 us
    reduce_scatter x9, waiting for transfers between devices, couple(): lax.psum_scatter(partial_value, 'scen', scatter_dimension=1, tiled=True)  92.3 us
    dot_general x9, matrix products, adjoint(): jnp.dot(rows_bf.reshape(batch, scen_local * rows), tech_flat, preferred_e...  87.1 us
    all_gather x9, blocking collectives, body(): lax.all_gather(dir_first.astype(bf16), 'scen', axis=1, tiled=True)  86.4 us
  transfers between devices with their start and end apart: 18, of which 12 were waited for; matrix products, arithmetic and copies ran while one was open for 2% of the time, Pallas kernels for 0%

commit v1 on v0

--- a/solution.py
+++ b/solution.py
@@ -61,7 +61,7 @@
         )
 
     def total_norm(first_vec, second_vec):
-        return lax.psum(local_squares(first_vec, second_vec), ("scen", "col"))
+        return lax.psum(lax.psum(local_squares(first_vec, second_vec), "col"), "scen")
 
     here_rows = rhs.shape[2]
     first_sol = jnp.zeros((batch, share_cols), f32)

time: 1610 us -> 1550 us (0.963)
  blocking collectives: 692 us -> 648 us
    psum x9 -> x18, blocking collectives: 355 us -> 198 us  [the longest x9 107 us: total_norm(): lax.psum(lax.psum(local_squares(first_vec, second_vec), 'col'), 'scen')]
    psum x6 -> x9, blocking collectives: 240 us -> 354 us  [body(): curv = lax.psum(curv_term, ('scen', 'col'))]
where the time goes in v1:
time: 1550 us; the launch traced here: 1540 us
  blocking collectives  648 us (42%)
  waiting for transfers between devices  542 us (35%)
  matrix products  292 us (19%)
  other arithmetic  39.5 us (3%)
  between operations  15.6 us (1%)
    psum x9, waiting for transfers between devices, body(): lax.psum(forward_partial_value + jnp.einsum('bsk,smk->bsm', dir_second.as...  449 us
    psum x9, blocking collectives, body(): curv = lax.psum(curv_term, ('scen', 'col'))  354 us
    dot_general x9, matrix products, body(): lax.dot_general(dir_first_bf, tech_flat, (((1,), (1,)), ((), ())), prefer...  107 us
    psum x9, blocking collectives, total_norm(): lax.psum(lax.psum(local_squares(first_vec, second_vec), 'col'), 'scen')  107 us
    reduce_scatter x9, waiting for transfers between devices, couple(): lax.psum_scatter(partial_value, 'scen', scatter_dimension=1, tiled=True)  92.3 us
    psum x9, blocking collectives, total_norm(): lax.psum(local_squares(first_vec, second_vec), 'col')  91.2 us
    dot_general x9, matrix products, adjoint(): jnp.dot(rows_bf.reshape(batch, scen_local * rows), tech_flat, preferred_e...  87.1 us
    all_gather x9, blocking collectives, body(): lax.all_gather(dir_first.astype(bf16), 'scen', axis=1, tiled=True)  86.1 us
  transfers between devices with their start and end apart: 18, of which 12 were waited for; matrix products, arithmetic and copies ran while one was open for 2% of the time, Pallas kernels for 0%

profile of v1, /device:TPU:0, one launch (start us, length us, event | category | flops | bytes accessed | tf_op | source)
XLA Modules:
  0.0 1542.6 jit_solution(11445897033024370043)
XLA Ops:
  22.1 32.4 %reduce-scatter.10.cloned.1.call-done = f32[32,128]{1,0:T(8,128)} async-done(((f32[32,1024]{1,0:T(8,128)}), f32[32,128]{1,0:T(8,128)}) %reduce-scatter.10.cloned.1.call-update) | async-done | bytes 16400 | tf_op jit(solution)/shard_map/reduce_scatter | solution.py:49
  64.2 12.0 fusion.136
  79.9 52.0 %all-reduce.11.cloned.1.call-done = f32[32,4,2048]{2,0,1:T(8,128)} async-done(((f32[32,4,2048]{2,0,1:T(8,128)}), f32[32,4,2048]{2,0,1:T(8,128)}) %all-reduce.11.cloned.1.call-update) | async-done | bytes 1048592 | tf_op jit(solution)/shard_map/psum | solution.py:85
  152.0 11.8 psum.253
  163.8 38.2 %psum.255 = f32[32]{0:T(128)S(1)} all-reduce(f32[32]{0:T(128)S(1)} %get-tuple-element.42), channel_id=1, replica_groups=mesh['scen'=8,'col'=4] {'scen','col'}, use_global_device_ids=true, to_apply=%region_7.0 | all-reduce | flops 32 | bytes 256 | tf_op jit(solution)/shard_map/psum | solution.py:95
  206.1 10.1 psum.256
  216.2 12.0 psum.257
  237.9 11.9 fusion.134
  253.6 49.2 %all-reduce.13.cloned.1.call-done = f32[32,4,2048]{2,0,1:T(8,128)} async-done(((f32[32,4,2048]{2,0,1:T(8,128)}), f32[32,4,2048]{2,0,1:T(8,128)}) %all-reduce.13.cloned.1.call-update) | async-done | bytes 1048592 | tf_op jit(solution)/shard_map/psum | solution.py:85
  314.1 40.0 %psum.259 = f32[32]{0:T(128)S(1)} all-reduce(f32[32]{0:T(128)S(1)} %multiply_add_fusion.27), channel_id=1, replica_groups=mesh['scen'=8,'col'=4] {'scen','col'}, use_global_device_ids=true, to_apply=%region_17.0 | all-reduce | flops 32 | bytes 256 | tf_op jit(solution)/shard_map/psum | solution.py:95
  358.2 10.2 psum.260
  368.4 11.8 psum.261
  381.2 10.1 all_gather.32
  391.3 11.9 fusion.132
  407.2 48.9 %all-reduce.15.cloned.1.call-done = f32[32,4,2048]{2,0,1:T(8,128)} async-done(((f32[32,4,2048]{2,0,1:T(8,128)}), f32[32,4,2048]{2,0,1:T(8,128)}) %all-reduce.15.cloned.1.call-update) | async-done | bytes 1048592 | tf_op jit(solution)/shard_map/psum | solution.py:85
  457.6 40.0 %psum.263 = f32[32]{0:T(128)S(1)} all-reduce(f32[32]{0:T(128)S(1)} %multiply_add_fusion.26), channel_id=1, replica_groups=mesh['scen'=8,'col'=4] {'scen','col'}, use_global_device_ids=true, to_apply=%region_27.0 | all-reduce | flops 32 | bytes 256 | tf_op jit(solution)/shard_map/psum | solution.py:95
  525.4 29.9 %reduce-scatter.16.cloned.1.call-done = f32[32,128]{1,0:T(8,128)} async-done(((f32[32,1024]{1,0:T(8,128)}), f32[32,128]{1,0:T(8,128)}) %reduce-scatter.16.cloned.1.call-update) | async-done | bytes 16400 | tf_op jit(solution)/shard_map/reduce_scatter | solution.py:49
  565.1 11.9 fusion.130
  580.6 52.0 %all-reduce.17.cloned.1.call-done = f32[32,4,2048]{2,0,1:T(8,128)} async-done(((f32[32,4,2048]{2,0,1:T(8,128)}), f32[32,4,2048]{2,0,1:T(8,128)}) %all-reduce.17.cloned.1.call-update) | async-done | bytes 1048592 | tf_op jit(solution)/shard_map/psum | solution.py:85
  652.8 11.8 psum.265
  664.6 38.0 %psum.267 = f32[32]{0:T(128)S(1)} all-reduce(f32[32]{0:T(128)S(1)} %get-tuple-element.32), channel_id=1, replica_groups=mesh['scen'=8,'col'=4] {'scen','col'}, use_global_device_ids=true, to_apply=%region_35.36 | all-reduce | flops 32 | bytes 256 | tf_op jit(solution)/shard_map/psum | solution.py:95
  706.6 10.1 psum.268
  716.8 11.9 psum.269
  738.7 11.9 fusion.128
  754.4 49.2 %all-reduce.19.cloned.1.call-done = f32[32,4,2048]{2,0,1:T(8,128)} async-done(((f32[32,4,2048]{2,0,1:T(8,128)}), f32[32,4,2048]{2,0,1:T(8,128)}) %all-reduce.19.cloned.1.call-update) | async-done | bytes 1048592 | tf_op jit(solution)/shard_map/psum | solution.py:85
  814.9 40.0 %psum.271 = f32[32]{0:T(128)S(1)} all-reduce(f32[32]{0:T(128)S(1)} %multiply_add_fusion.24), channel_id=1, replica_groups=mesh['scen'=8,'col'=4] {'scen','col'}, use_global_device_ids=true, to_apply=%region_45.46 | all-reduce | flops 32 | bytes 256 | tf_op jit(solution)/shard_map/psum | solution.py:95
  859.0 10.2 psum.272
  869.2 11.8 psum.273
  882.5 10.1 all_gather.35
  892.6 11.9 fusion.126
  908.4 49.1 %all-reduce.21.cloned.1.call-done = f32[32,4,2048]{2,0,1:T(8,128)} async-done(((f32[32,4,2048]{2,0,1:T(8,128)}), f32[32,4,2048]{2,0,1:T(8,128)}) %all-reduce.21.cloned.1.call-update) | async-done | bytes 1048592 | tf_op jit(solution)/shard_map/psum | solution.py:85
  958.9 40.0 %psum.275 = f32[32]{0:T(128)S(1)} all-reduce(f32[32]{0:T(128)S(1)} %multiply_add_fusion.23), channel_id=1, replica_groups=mesh['scen'=8,'col'=4] {'scen','col'}, use_global_device_ids=true, to_apply=%region_55.56 | all-reduce | flops 32 | bytes 256 | tf_op jit(solution)/shard_map/psum | solution.py:95
  1028.1 29.9 %reduce-scatter.22.cloned.1.call-done = f32[32,128]{1,0:T(8,128)} async-done(((f32[32,1024]{1,0:T(8,128)}), f32[32,128]{1,0:T(8,128)}) %reduce-scatter.22.cloned.1.call-update) | async-done | bytes 16400 | tf_op jit(solution)/shard_map/reduce_scatter | solution.py:49
  1067.8 11.9 fusion.124
  1083.3 52.0 %all-reduce.23.cloned.1.call-done = f32[32,4,2048]{2,0,1:T(8,128)} async-done(((f32[32,4,2048]{2,0,1:T(8,128)}), f32[32,4,2048]{2,0,1:T(8,128)}) %all-reduce.23.cloned.1.call-update) | async-done | bytes 1048592 | tf_op jit(solution)/shard_map/psum | solution.py:85
  1155.5 11.8 psum.277
  1167.3 38.0 %psum.279 = f32[32]{0:T(128)S(1)} all-reduce(f32[32]{0:T(128)S(1)} %get-tuple-element.18), channel_id=1, replica_groups=mesh['scen'=8,'col'=4] {'scen','col'}, use_global_device_ids=true, to_apply=%region_63.64 | all-reduce | flops 32 | bytes 256 | tf_op jit(solution)/shard_map/psum | solution.py:95
  1209.3 10.1 psum.280
  1219.4 11.9 psum.281
  1241.3 11.9 fusion.122
  1257.1 49.2 %all-reduce.25.cloned.1.call-done = f32[32,4,2048]{2,0,1:T(8,128)} async-done(((f32[32,4,2048]{2,0,1:T(8,128)}), f32[32,4,2048]{2,0,1:T(8,128)}) %all-reduce.25.cloned.1.call-update) | async-done | bytes 1048592 | tf_op jit(solution)/shard_map/psum | solution.py:85
  1317.7 40.0 %psum.283 = f32[32]{0:T(128)S(1)} all-reduce(f32[32]{0:T(128)S(1)} %multiply_add_fusion.21), channel_id=1, replica_groups=mesh['scen'=8,'col'=4] {'scen','col'}, use_global_device_ids=true, to_apply=%region_73.74 | all-reduce | flops 32 | bytes 256 | tf_op jit(solution)/shard_map/psum | solution.py:95
  1361.7 10.2 psum.284
  1372.0 11.8 psum.285
  1395.8 11.9 fusion.120
  1413.1 47.5 %all-reduce.27.cloned.1.call-done = f32[32,4,2048]{2,0,1:T(8,128)} async-done(((f32[32,4,2048]{2,0,1:T(8,128)}), f32[32,4,2048]{2,0,1:T(8,128)}) %all-reduce.27.cloned.1.call-update) | async-done | bytes 1048592 | tf_op jit(solution)/shard_map/psum | solution.py:85
  1463.2 40.1 %psum.287 = f32[32]{0:T(128)} all-reduce(f32[32]{0:T(128)} %multiply_add_fusion.20), channel_id=1, replica_groups=mesh['scen'=8,'col'=4] {'scen','col'}, use_global_device_ids=true, to_apply=%region_83.84 | all-reduce | flops 32 | bytes 256 | tf_op jit(solution)/shard_map/psum | solution.py:95
  1506.3 10.3 all_gather.39
  (288 shorter events, 326.5 us)
Async XLA Ops:
  7.2 47.4 %reduce-scatter.10.cloned.1.call-start = ((), (), s32[]{:S(2)}) async-start(), calls=%async_computation.9 | async-start | bytes 147456 | tf_op jit(solution)/shard_map/reduce_scatter | solution.py:49
  18.1 113.7 %all-reduce.11.cloned.1.call-start = ((), (), s32[]{:S(2)}) async-start(), calls=%async_computation.10 | async-start | bytes 2097152 | tf_op jit(solution)/shard_map/psum | solution.py:85
  18.9 1212.4 %copy-start.43 = (f32[128]{0:T(128)}, f32[128]{0:T(128)S(1)}, u32[]{:S(2)}) copy-start(f32[128]{0:T(128)S(1)} %dynamic_slice.9) | copy-start | bytes 1540
  22.1 227.7 %copy-start.24 = (f32[32,4,256]{2,0,1:T(8,128)}, f32[32,4,256]{2,0,1:T(8,128)S(1)}, u32[]{:S(2)}) copy-start(f32[32,4,256]{2,0,1:T(8,128)S(1)} %get-tuple-element.54) | copy-start | bytes 393220
  79.8 125.3 %reduce-scatter.12.cloned.1.call-start = ((), (), s32[]{:S(2)}) async-start(), calls=%async_computation.11 | async-start | bytes 147456 | tf_op jit(solution)/shard_map/reduce_scatter | solution.py:49
  141.7 63.5 %copy-start.37 = (f32[32,128]{1,0:T(8,128)S(1)}, f32[32,128]{1,0:T(8,128)}, u32[]{:S(2)}) copy-start(f32[32,128]{1,0:T(8,128)} %reduce-scatter.10.cloned.1.call-done) | copy-start | bytes 49156
  141.7 161.1 %all-reduce.13.cloned.1.call-start = ((), (), s32[]{:S(2)}) async-start(), calls=%async_computation.12 | async-start | bytes 2097152 | tf_op jit(solution)/shard_map/psum | solution.py:85
  202.0 295.6 %copy-start.49 = (f32[32]{0:T(128)}, f32[32]{0:T(128)S(1)}, u32[]{:S(2)}) copy-start(f32[32]{0:T(128)S(1)} %div.54) | copy-start | bytes 388
  253.6 103.7 %reduce-scatter.14.cloned.1.call-start = ((), (), s32[]{:S(2)}) async-start(), calls=%async_computation.13 | async-start | bytes 147456 | tf_op jit(solution)/shard_map/reduce_scatter | solution.py:49
  304.3 49.9 %copy-start.20 = (f32[32,4,2048]{2,0,1:T(8,128)S(1)}, f32[32,4,2048]{2,0,1:T(8,128)}, u32[]{:S(2)}) copy-start(f32[32,4,2048]{2,0,1:T(8,128)} %all-reduce.13.cloned.1.call-done) | copy-start | bytes 3145732
  314.1 142.0 %all-reduce.15.cloned.1.call-start = ((), (), s32[]{:S(2)}) async-start(), calls=%async_computation.14 | async-start | bytes 2097152 | tf_op jit(solution)/shard_map/psum | solution.py:85
  354.1 143.5 %copy-start.46 = (f32[32]{0:T(128)}, f32[32]{0:T(128)S(1)}, u32[]{:S(2)}) copy-start(f32[32]{0:T(128)S(1)} %div.56) | copy-start | bytes 388
  357.2 49.8 %copy-start.27 = (f32[32,4,256]{2,0,1:T(8,128)}, f32[32,4,256]{2,0,1:T(8,128)S(1)}, u32[]{:S(2)}) copy-start(f32[32,4,256]{2,0,1:T(8,128)S(1)} %get-tuple-element.58) | copy-start | bytes 393220
  380.2 26.8 %copy-start.52 = (f32[32]{0:T(128)}, f32[32]{0:T(128)S(1)}, u32[]{:S(2)}) copy-start(f32[32]{0:T(128)S(1)} %div.57) | copy-start | bytes 388
  406.7 93.0 %copy-start.9 = (f32[32,4,2048]{2,1,0:T(4,128)S(1)}, f32[32,4,2048]{2,1,0:T(4,128)}, u32[]{:S(2)}) copy-start(f32[32,4,2048]{2,1,0:T(4,128)} %param.8) | copy-start | bytes 3145732
  406.8 148.5 %reduce-scatter.16.cloned.1.call-start = ((), (), s32[]{:S(2)}) async-start(), calls=%async_computation.15 | async-start | bytes 147456 | tf_op jit(solution)/shard_map/reduce_scatter | solution.py:49
  407.0 600.6 %copy-start.44 = (f32[4,2048]{1,0:T(4,128)}, f32[4,2048]{1,0:T(4,128)S(1)}, u32[]{:S(2)}) copy-start(f32[4,2048]{1,0:T(4,128)S(1)} %broadcast_subtract_fusion) | copy-start | bytes 98308
  457.6 553.4 %copy-start.35 = (f32[4,2048]{1,0:T(4,128)}, f32[4,2048]{1,0:T(4,128)S(1)}, u32[]{:S(2)}) copy-start(f32[4,2048]{1,0:T(4,128)S(1)} %pad_convert_fusion) | copy-start | bytes 98308
  522.2 110.4 %all-reduce.17.cloned.1.call-start = ((), (), s32[]{:S(2)}) async-start(), calls=%async_computation.16 | async-start | bytes 2097152 | tf_op jit(solution)/shard_map/psum | solution.py:85
  525.4 225.2 %copy-start.25 = (f32[32,4,256]{2,0,1:T(8,128)}, f32[32,4,256]{2,0,1:T(8,128)S(1)}, u32[]{:S(2)}) copy-start(f32[32,4,256]{2,0,1:T(8,128)S(1)} %get-tuple-element.64) | copy-start | bytes 393220
  580.6 125.1 %reduce-scatter.18.cloned.1.call-start = ((), (), s32[]{:S(2)}) async-start(), calls=%async_computation.17 | async-start | bytes 147456 | tf_op jit(solution)/shard_map/reduce_scatter | solution.py:49
  642.5 63.3 %copy-start.38 = (f32[32,128]{1,0:T(8,128)S(1)}, f32[32,128]{1,0:T(8,128)}, u32[]{:S(2)}) copy-start(f32[32,128]{1,0:T(8,128)} %reduce-scatter.16.cloned.1.call-done) | copy-start | bytes 49156
  642.5 161.1 %all-reduce.19.cloned.1.call-start = ((), (), s32[]{:S(2)}) async-start(), calls=%async_computation.18 | async-start | bytes 2097152 | tf_op jit(solution)/shard_map/psum | solution.py:85
  702.6 296.3 %copy-start.50 = (f32[32]{0:T(128)}, f32[32]{0:T(128)S(1)}, u32[]{:S(2)}) copy-start(f32[32]{0:T(128)S(1)} %div.60) | copy-start | bytes 388
  728.9 152.1 %copy-start.33 = (f32[32,128]{1,0:T(8,128)}, f32[32,128]{1,0:T(8,128)S(1)}, u32[]{:S(2)}) copy-start(f32[32,128]{1,0:T(8,128)S(1)} %get-tuple-element.29) | copy-start | bytes 49156
  754.3 103.7 %reduce-scatter.20.cloned.1.call-start = ((), (), s32[]{:S(2)}) async-start(), calls=%async_computation.19 | async-start | bytes 147456 | tf_op jit(solution)/shard_map/reduce_scatter | solution.py:49
  805.0 49.9 %copy-start.21 = (f32[32,4,2048]{2,0,1:T(8,128)S(1)}, f32[32,4,2048]{2,0,1:T(8,128)}, u32[]{:S(2)}) copy-start(f32[32,4,2048]{2,0,1:T(8,128)} %all-reduce.19.cloned.1.call-done) | copy-start | bytes 3145732
  814.9 142.6 %all-reduce.21.cloned.1.call-start = ((), (), s32[]{:S(2)}) async-start(), calls=%async_computation.20 | async-start | bytes 2097152 | tf_op jit(solution)/shard_map/psum | solution.py:85
  854.9 144.0 %copy-start.47 = (f32[32]{0:T(128)}, f32[32]{0:T(128)S(1)}, u32[]{:S(2)}) copy-start(f32[32]{0:T(128)S(1)} %div.62) | copy-start | bytes 388
  858.0 50.2 %copy-start.28 = (f32[32,4,256]{2,0,1:T(8,128)}, f32[32,4,256]{2,0,1:T(8,128)S(1)}, u32[]{:S(2)}) copy-start(f32[32,4,256]{2,0,1:T(8,128)S(1)} %get-tuple-element.68) | copy-start | bytes 393220
  881.0 27.2 %copy-start.53 = (f32[32]{0:T(128)}, f32[32]{0:T(128)S(1)}, u32[]{:S(2)}) copy-start(f32[32]{0:T(128)S(1)} %div.63) | copy-start | bytes 388
  908.2 149.8 %reduce-scatter.22.cloned.1.call-start = ((), (), s32[]{:S(2)}) async-start(), calls=%async_computation.21 | async-start | bytes 147456 | tf_op jit(solution)/shard_map/reduce_scatter | solution.py:49
  1024.9 110.4 %all-reduce.23.cloned.1.call-start = ((), (), s32[]{:S(2)}) async-start(), calls=%async_computation.22 | async-start | bytes 2097152 | tf_op jit(solution)/shard_map/psum | solution.py:85
  1028.1 225.2 %copy-start.26 = (f32[32,4,256]{2,0,1:T(8,128)}, f32[32,4,256]{2,0,1:T(8,128)S(1)}, u32[]{:S(2)}) copy-start(f32[32,4,256]{2,0,1:T(8,128)S(1)} %get-tuple-element.72) | copy-start | bytes 393220
  1083.3 125.1 %reduce-scatter.24.cloned.1.call-start = ((), (), s32[]{:S(2)}) async-start(), calls=%async_computation.23 | async-start | bytes 147456 | tf_op jit(solution)/shard_map/reduce_scatter | solution.py:49
  1145.1 63.3 %copy-start.39 = (f32[32,128]{1,0:T(8,128)S(1)}, f32[32,128]{1,0:T(8,128)}, u32[]{:S(2)}) copy-start(f32[32,128]{1,0:T(8,128)} %reduce-scatter.22.cloned.1.call-done) | copy-start | bytes 49156
  1145.2 161.2 %all-reduce.25.cloned.1.call-start = ((), (), s32[]{:S(2)}) async-start(), calls=%async_computation.24 | async-start | bytes 2097152 | tf_op jit(solution)/shard_map/psum | solution.py:85
  1205.3 26.1 %copy-start.51 = (f32[32]{0:T(128)}, f32[32]{0:T(128)S(1)}, u32[]{:S(2)}) copy-start(f32[32]{0:T(128)S(1)} %div.66) | copy-start | bytes 388
  1231.6 152.2 %copy-start.34 = (f32[32,128]{1,0:T(8,128)}, f32[32,128]{1,0:T(8,128)S(1)}, u32[]{:S(2)}) copy-start(f32[32,128]{1,0:T(8,128)S(1)} %get-tuple-element.15) | copy-start | bytes 49156
  1257.1 103.7 %reduce-scatter.26.cloned.1.call-start = ((), (), s32[]{:S(2)}) async-start(), calls=%async_computation.25 | async-start | bytes 147456 | tf_op jit(solution)/shard_map/reduce_scatter | solution.py:49
  1307.8 49.9 %copy-start.18 = (f32[32,4,2048]{2,0,1:T(8,128)S(1)}, f32[32,4,2048]{2,0,1:T(8,128)}, u32[]{:S(2)}) copy-start(f32[32,4,2048]{2,0,1:T(8,128)} %all-reduce.25.cloned.1.call-done) | copy-start | bytes 3145732
  1317.6 143.0 %all-reduce.27.cloned.1.call-start = ((), (), s32[]{:S(2)}) async-start(), calls=%async_computation.26 | async-start | bytes 2097152 | tf_op jit(solution)/shard_map/psum | solution.py:85
  1357.6 50.1 %copy-start.48 = (f32[32]{0:T(128)}, f32[32]{0:T(128)S(1)}, u32[]{:S(2)}) copy-start(f32[32]{0:T(128)S(1)} %div.68) | copy-start | bytes 388
  1360.8 47.0 %copy-start.29 = (f32[32,4,256]{2,0,1:T(8,128)}, f32[32,4,256]{2,0,1:T(8,128)S(1)}, u32[]{:S(2)}) copy-start(f32[32,4,256]{2,0,1:T(8,128)S(1)} %get-tuple-element.76) | copy-start | bytes 393220
  1383.7 24.0 %copy-start.57 = (f32[32]{0:T(128)}, f32[32]{0:T(128)S(1)}, u32[]{:S(2)}) copy-start(f32[32]{0:T(128)S(1)} %psum.285) | copy-start | bytes 388
  1411.3 106.0 %copy-start.11 = (f32[32,4,2048]{2,1,0:T(4,128)S(1)}, f32[32,4,2048]{2,1,0:T(4,128)}, u32[]{:S(2)}) copy-start(f32[32,4,2048]{2,1,0:T(4,128)} %param.8) | copy-start | bytes 3145732
  1411.3 106.0 %copy-start.15 = (f32[32,4,2048]{2,0,1:T(8,128)S(1)}, f32[32,4,2048]{2,0,1:T(8,128)}, u32[]{:S(2)}) copy-start(f32[32,4,2048]{2,0,1:T(8,128)} %all-reduce.23.cloned.1.call-done) | copy-start | bytes 3145732
  1411.3 106.0 %copy-start.19 = (f32[32,4,2048]{2,0,1:T(8,128)S(1)}, f32[32,4,2048]{2,0,1:T(8,128)}, u32[]{:S(2)}) copy-start(f32[32,4,2048]{2,0,1:T(8,128)} %all-reduce.25.cloned.1.call-done) | copy-start | bytes 3145732
  (28 other events, 255.4 us)
Sparse Core Ops, SparseCore 0:
  18.2 36.2 reduce-scatter.9
  79.9 51.8 all-reduce.10
  141.8 32.8 reduce-scatter.11
  253.7 49.1 all-reduce.12
  314.2 32.8 reduce-scatter.13
  406.9 49.1 all-reduce.14
  522.3 32.8 reduce-scatter.15
  580.7 51.9 all-reduce.16
  642.6 32.8 reduce-scatter.17
  754.5 49.1 all-reduce.18
  815.0 32.8 reduce-scatter.19
  908.3 49.1 all-reduce.20
  1025.0 32.8 reduce-scatter.21
  1083.4 51.8 all-reduce.22
  1145.3 32.8 reduce-scatter.23
  1257.2 49.0 all-reduce.24
  1317.7 32.8 reduce-scatter.25
  1411.5 49.1 all-reduce.26
